TPU v7x, 512 devices: a whole 4x8x8 slice. The times are simulated.
512 devices in a mesh: date: 64 (over z, y), pix: 8 (over x, core).
Axes of the slice: x: 4, y: 8, z: 8, core: 2. Of those that a mesh axis runs over, the one named last changes fastest.
Arguments:
- reflect: bfloat16 [64, 6, 65536], P('date', None, 'pix'), may hold values from -8 to 8
- cloud_free: int32 [64, 65536], P('date', 'pix'), may hold values from 0 to 1, as said below
- days: int32 [64], P('date'), may hold values from 1 to 2079, as said below
Outputs:
- median: float32 [6, 65536], P(None, 'pix')
- slope: float32 [6, 65536], P(None, 'pix')
Inputs may be any that keep to these rules, and one draw needn't show every extreme that they name: `cloud_free`: every pixel is clear on at least one of the first 32 dates and on at least one of the others; clear shares differ between tiles. `days`: strictly increasing.
All inputs are finite; a program needn't handle non-finite values.
Results may differ from a plain program's by a relative error of at most 0.0003.
Values may be sent and summed in bfloat16 or wider, within the bound.
A program may use at most 64 MiB of HBM per device.

v0:
```python
import math

import jax
import jax.numpy as jnp
from jax import lax
from jax.sharding import Mesh
from jax.sharding import PartitionSpec as P

DATE = ("date_0", "date_1")


ridge = 1.0
sentinel = 100.0


def from_everyone(x, axis):
    copies = jnp.broadcast_to(x, (lax.axis_size(axis), *x.shape))
    return lax.all_to_all(copies, axis, split_axis=0, concat_axis=0, tiled=True)


def taken_together(x, axis):
    everything = from_everyone(x, axis)
    return jnp.sum(everything, axis=0)


def packed_total(arrays, axis):
    ends = [0]
    for a in arrays:
        ends.append(ends[-1] + a.size)
    running = taken_together(jnp.concatenate([a.ravel() for a in arrays]), axis)
    return tuple((running[b:e].reshape(a.shape) for a, b, e in zip(arrays, ends, ends[1:])))


def cut_along(x, dim, peers):
    before, after = (x.shape[:dim], x.shape[dim + 1 :])
    return jnp.moveaxis(x.reshape(*before, peers, -1, *after), dim, 0)


def in_order(pieces, dim):
    pieces = jnp.moveaxis(pieces, 0, dim)
    shape = pieces.shape
    return pieces.reshape(*shape[:dim], shape[dim] * shape[dim + 1], *shape[dim + 2 :])


def turned_blocks(pieces, axes, sequence):
    inside = pieces.shape[1:]
    out = pieces.reshape(*(lax.axis_size(a) for a in axes), *inside)
    for k in sequence:
        out = lax.all_to_all(out, axes[k], k, k, tiled=True)
    return out.reshape(-1, *inside)


def exchange_by_axis(x, axes, sequence, split_dim, concat_dim):
    pieces = cut_along(x, split_dim, lax.axis_size(axes))
    return in_order(turned_blocks(pieces, axes, sequence), concat_dim)


def side_by_side(arrays, axis, dim, along):
    widths = [math.prod(a.shape[along:]) for a in arrays]
    both = jnp.concatenate(
        [a.reshape(*a.shape[:along], w) for a, w in zip(arrays, widths)], axis=along
    )
    out = lax.all_gather(both, axis, axis=dim, tiled=True)
    pieces = jnp.split(out, [sum(widths[:k]) for k in range(1, len(widths))], axis=along)
    return tuple((b.reshape(*out.shape[:along], *a.shape[along:]) for a, b in zip(arrays, pieces)))


def sent_together(arrays, axis, dim, along):
    both = jnp.concatenate(arrays, axis=along)
    out, at, finished = (lax.all_gather(both, axis, axis=dim, tiled=True), 0, [])
    for a in arrays:
        finished.append(lax.slice_in_dim(out, at, at + a.shape[along], axis=along))
        at += a.shape[along]
    return tuple(finished)


def count_ranks(carry, own, piece):

    def step(i, state):
        less, equal, count = state
        other = lax.dynamic_index_in_dim(piece, i, 0, keepdims=True).astype(jnp.float32)
        less = less + (other < own).astype(jnp.float32)
        equal = equal + (other == own).astype(jnp.float32)
        count = count + (other[0, 0] < 50.0).astype(jnp.float32)
        return (less, equal, count)

    return lax.fori_loop(0, piece.shape[0], step, carry)


def select_sums(values, valid, less, equal, count):
    lower = jnp.floor((count - 1.0) / 2.0)
    upper = jnp.floor(count / 2.0)
    low_pick = valid[:, None, :] * ((less <= lower) & (lower < less + equal)).astype(jnp.float32)
    high_pick = valid[:, None, :] * ((less <= upper) & (upper < less + equal)).astype(jnp.float32)
    return (
        jnp.sum(low_pick * values, 0),
        jnp.sum(low_pick, 0),
        jnp.sum(high_pick * values, 0),
        jnp.sum(high_pick, 0),
    )


def finish_median(low_num, low_den, high_num, high_den):
    return 0.5 * (low_num / jnp.maximum(low_den, 1.0) + high_num / jnp.maximum(high_den, 1.0))


def column_median(moved):
    column = moved.astype(jnp.float32)
    column_valid = (column[:, 0, :] < 50.0).astype(jnp.float32)
    zeros = jnp.zeros(column.shape, jnp.float32)
    start_carry = (zeros, zeros, jnp.zeros((column.shape[2],), jnp.float32))
    less, equal, count = count_ranks(start_carry, column, moved)
    low_num, low_den, high_num, high_den = select_sums(column, column_valid, less, equal, count)
    return (column, column_valid, finish_median(low_num, low_den, high_num, high_den))


def fit_slope(s_zero, s_one, s_two, s_y, s_ty):
    first = s_zero + ridge
    determinant = first * (s_two + ridge) - s_one * s_one
    return (first[None, :] * s_ty - s_one[None, :] * s_y) / determinant[None, :]


def local(reflect, cloud_free, days):
    values = reflect.astype(jnp.float32)
    valid = cloud_free.astype(jnp.float32)
    years = days.astype(jnp.float32) / 365.0
    csum = jnp.sum(values * valid[:, None, :], 2)
    cnt = jnp.sum(valid, 1)
    csum, cnt = packed_total((csum, cnt), "pix")
    scene_mean = csum / jnp.maximum(cnt, 1.0)[:, None]
    marked = jnp.where(valid[:, None, :] > 0, values, sentinel).astype(jnp.bfloat16)
    moved = exchange_by_axis(marked, DATE, (0, 1), 2, 0)
    column, column_valid, part_median = column_median(moved)
    all_means, all_years = side_by_side((scene_mean, years), DATE, 0, 1)
    weighted = column_valid[:, None, :] * (column - all_means[:, :, None])
    s_zero = jnp.sum(column_valid, 0)
    s_one = jnp.sum(all_years[:, None] * column_valid, 0)
    s_two = jnp.sum((all_years * all_years)[:, None] * column_valid, 0)
    s_y = jnp.sum(weighted, 0)
    s_ty = jnp.sum(all_years[:, None, None] * weighted, 0)
    part_slope = fit_slope(s_zero, s_one, s_two, s_y, s_ty)
    median, slope = sent_together((part_median, part_slope), DATE, 1, 0)
    return (median, slope)


def solution(mesh):
    torus = Mesh(mesh.devices.reshape(8, 8, mesh.shape["pix"]), ("date_0", "date_1", "pix"))
    return jax.shard_map(
        local,
        mesh=torus,
        in_specs=(P(DATE, None, "pix"), P(DATE, "pix"), P(DATE)),
        out_specs=(P(None, "pix"), P(None, "pix")),
        check_vma=False,
    )
```

profile of v0, /device:TPU:8, one launch (start us, length us, event | category | flops | bytes accessed | tf_op | source)
XLA Modules:
  0.0 148.9 jit_solution(10980949815485690425)
XLA Ops:
  0.6 1.5 convert_reduce_fusion.1
  2.1 0.8 convert_element_type.58
  2.9 0.2 fusion.4
  3.1 0.7 pad_maximum_fusion.1
  3.8 0.6 broadcast_in_dim.25
  4.4 4.3 %all-to-all-start.2 = ((f32[8,1,7]{2,1,0:T(1,128)}), f32[8,1,7]{2,1,0:T(1,128)S(1)}, u32[]{:S(2)}, u32[]{:S(2)}) async-start(f32[8,1,7]{2,1,0:T(1,128)} %broadcast_in_dim.25), calls=%async_computation.2 | async-start | bytes 8192 | tf_op jit(solution)/shard_map/all_to_all | solution.py:18
  9.4 0.7 copy.61
  10.1 3.9 %all-to-all-done.2 = f32[8,1,7]{2,1,0:T(1,128)S(1)} async-done(((f32[8,1,7]{2,1,0:T(1,128)}), f32[8,1,7]{2,1,0:T(1,128)S(1)}, u32[]{:S(2)}, u32[]{:S(2)}) %all-to-all-start.2) | async-done | bytes 256 | tf_op jit(solution)/shard_map/all_to_all | solution.py:18
  13.9 10.3 %all-to-all-start = ((bf16[8,8,1,6,128]{4,1,3,2,0:T(8,128)(2,1)}), bf16[8,8,1,6,128]{4,1,3,2,0:T(8,128)(2,1)S(1)}, u32[]{:S(2)}, u32[]{:S(2)}) async-start(bf16[8,8,1,6,128]{4,1,3,2,0:T(8,128)(2,1)} %copy.61), calls=%async_computation | async-start | bytes 196608 | tf_op jit(solution)/shard_map/all_to_all | solution.py:49
  24.3 0.6 slice.24
  25.6 45.4 %all-gather = f32[64,1,7]{2,1,0:T(1,128)S(1)} all-gather(f32[1,1,7]{2,1,0:T(1,128)S(1)} %maximum_bitcast_fusion), channel_id=1, replica_groups=mesh['date_0'=8,'date_1'=8,'pix'=8] {'date_0','date_1'}, dimensions={0}, use_global_device_ids=true | all-gather | bytes 1820 | tf_op jit(solution)/shard_map/all_gather | solution.py:63
  71.1 0.7 copy.62
  71.7 5.8 %all-to-all-start.1 = ((bf16[8,8,1,6,128]{4,0,3,2,1:T(8,128)(2,1)}), bf16[8,8,1,6,128]{4,0,3,2,1:T(8,128)(2,1)S(1)}, u32[]{:S(2)}, u32[]{:S(2)}) async-start(bf16[8,8,1,6,128]{4,0,3,2,1:T(8,128)(2,1)} %copy.62), calls=%async_computation.1 | async-start | bytes 196608 | tf_op jit(solution)/shard_map/all_to_all | solution.py:49
  77.7 0.2 multiply_reduce_fusion.1
  78.0 6.8 %all-to-all-done.1 = bf16[8,8,1,6,128]{4,0,3,2,1:T(8,128)(2,1)S(1)} async-done(((bf16[8,8,1,6,128]{4,0,3,2,1:T(8,128)(2,1)}), bf16[8,8,1,6,128]{4,0,3,2,1:T(8,128)(2,1)S(1)}, u32[]{:S(2)}, u32[]{:S(2)}) %all-to-all-start.1) | async-done | bytes 98336 | tf_op jit(solution)/shard_map/all_to_all | solution.py:49
  85.2 14.3 %while.18 = (s32[]{:T(128)}, f32[64,6,128]{2,1,0:T(8,128)S(1)}, f32[64,6,128]{2,1,0:T(8,128)S(1)}, f32[128]{0:T(128)S(1)}, bf16[64,6,128]{2,1,0:T(8,128)(2,1)S(1...) while((s32[]{:T(128)}, f32[64,6,128]{2,1,0:T(8,128)S(1)}, f32[64,6,128]{2,1,0:T(8,128)S(1)}, ...), condition=%wide.region_1.0_spmd.clone, body=%wide.region_0.0_spmd.clone.sunk | while | flops 394499 | bytes 995436 | solution.py:87
  85.2 0.2 select_add_fusion.3
  85.7 0.2 select_add_fusion.3
  85.9 0.2 select_add_fusion.3
  86.1 0.2 select_add_fusion.3
  86.4 0.2 select_add_fusion.3
  86.8 0.2 select_add_fusion.3
  87.0 0.2 select_add_fusion.3
  87.3 0.2 select_add_fusion.3
  87.5 0.2 select_add_fusion.3
  87.9 0.2 select_add_fusion.3
  88.2 0.2 select_add_fusion.3
  88.4 0.2 select_add_fusion.3
  88.8 0.2 select_add_fusion.3
  89.0 0.2 select_add_fusion.3
  89.3 0.2 select_add_fusion.3
  89.5 0.2 select_add_fusion.3
  89.9 0.2 select_add_fusion.3
  90.2 0.2 select_add_fusion.3
  90.4 0.2 select_add_fusion.3
  90.6 0.2 select_add_fusion.3
  91.1 0.2 select_add_fusion.3
  91.3 0.2 select_add_fusion.3
  91.5 0.2 select_add_fusion.3
  91.7 0.2 select_add_fusion.3
  92.2 0.2 select_add_fusion.3
  92.4 0.2 select_add_fusion.3
  92.6 0.2 select_add_fusion.3
  93.1 0.2 select_add_fusion.3
  93.3 0.2 select_add_fusion.3
  93.5 0.2 select_add_fusion.3
  100.0 48.1 %all_gather.7 = f32[12,8192]{1,0:T(8,128)S(1)} all-gather(f32[12,128]{1,0:T(8,128)S(1)} %pad_maximum_fusion), channel_id=1, replica_groups=mesh['date_0'=8,'date_1'=8,'pix'=8] {'date_0','date_1'}, dimensions={1}, use_global_device_ids=true | all-gather | bytes 399360 | tf_op jit(solution)/shard_map/all_gather | solution.py:70
  148.0 0.8 fusion.10
  (191 shorter events, 8.3 us)
Async XLA Ops:
  0.6 2.3 %copy-start = (bf16[1,6,8192]{2,1,0:T(8,128)(2,1)S(1)}, bf16[1,6,8192]{2,1,0:T(8,128)(2,1)}, u32[]{:S(2)}) copy-start(bf16[1,6,8192]{2,1,0:T(8,128)(2,1)} %param.5) | copy-start | bytes 294916
  4.4 9.5 %all-to-all-start.2 = ((f32[8,1,7]{2,1,0:T(1,128)}), f32[8,1,7]{2,1,0:T(1,128)S(1)}, u32[]{:S(2)}, u32[]{:S(2)}) async-start(f32[8,1,7]{2,1,0:T(1,128)} %broadcast_in_dim.25), calls=%async_computation.2 | async-start | bytes 8192 | tf_op jit(solution)/shard_map/all_to_all | solution.py:18
  13.9 57.1 %all-to-all-start = ((bf16[8,8,1,6,128]{4,1,3,2,0:T(8,128)(2,1)}), bf16[8,8,1,6,128]{4,1,3,2,0:T(8,128)(2,1)S(1)}, u32[]{:S(2)}, u32[]{:S(2)}) async-start(bf16[8,8,1,6,128]{4,1,3,2,0:T(8,128)(2,1)} %copy.61), calls=%async_computation | async-start | bytes 196608 | tf_op jit(solution)/shard_map/all_to_all | solution.py:49
  71.7 13.1 %all-to-all-start.1 = ((bf16[8,8,1,6,128]{4,0,3,2,1:T(8,128)(2,1)}), bf16[8,8,1,6,128]{4,0,3,2,1:T(8,128)(2,1)S(1)}, u32[]{:S(2)}, u32[]{:S(2)}) async-start(bf16[8,8,1,6,128]{4,0,3,2,1:T(8,128)(2,1)} %copy.62), calls=%async_computation.1 | async-start | bytes 196608 | tf_op jit(solution)/shard_map/all_to_all | solution.py:49
where the time goes:
time: 149 us
  blocking collectives  93.5 us (63%)
  starting transfers between devices  20.4 us (14%)
  other arithmetic  16.2 us (11%)
  waiting for transfers between devices  10.7 us (7%)
  local copies, waits for them, and re-layouts  3.84 us (3%)
  loops' own time  2.15 us (1%)
  between operations  2.08 us (1%)
    all_gather x1, blocking collectives, sent_together(): lax.all_gather(both, axis, axis=dim, tiled=True)  48.1 us
    all_gather x1, blocking collectives, side_by_side(): out = lax.all_gather(both, axis, axis=dim, tiled=True)  45.4 us
    all_to_all x2, starting transfers between devices, turned_blocks(): out = lax.all_to_all(out, axes[k], k, k, tiled=True)  16.1 us
    add x64, other arithmetic, step(): equal = equal + (other == own).astype(jnp.float32)  10.6 us
    all_to_all x2, waiting for transfers between devices, turned_blocks(): out = lax.all_to_all(out, axes[k], k, k, tiled=True)  6.8 us
    all_to_all x1, starting transfers between devices, from_everyone(): return lax.all_to_all(copies, axis, split_axis=0, concat_axis=0, tiled=True)  4.3 us
    all_to_all x1, waiting for transfers between devices, from_everyone(): return lax.all_to_all(copies, axis, split_axis=0, concat_axis=0, tiled=True)  3.87 us
  transfers between devices with their start and end apart: 3, of which 2 were waited for; matrix products, arithmetic and copies ran while one was open for 1% of the time, Pallas kernels for 0%

commit v1 on v0

v1 whole, which is shorter than its diff:
```python
import functools

import jax
import jax.numpy as jnp
from jax import lax
from jax.experimental import pallas as pl
from jax.experimental.pallas import tpu as pltpu
from jax.sharding import Mesh
from jax.sharding import PartitionSpec as P

MESH = pl.DeviceIdType.MESH
DATE = ("date_0", "date_1")
SIDE = 8
DATES = SIDE * SIDE
PEERS = 8
LANES = 128
TILE = 8192
HALF = SIDE // 2
WORKERS = HALF * SIDE
WIDTH = TILE // WORKERS
CHUNKS = TILE // LANES
BANDS = 6
KEPT = DATES // 2 + 1
sentinel = 100.0
per_year = 1.0 / 365.0


def merged(lo, hi, r):
    step = 2 * r
    if step < hi - lo:
        yield from merged(lo, hi, step)
        yield from merged(lo + r, hi, step)
        yield from ((i, i + r) for i in range(lo + r, hi - r, step))
    else:
        yield (lo, lo + r)


def sorted_pairs(lo, hi):
    if hi > lo:
        mid = lo + (hi - lo) // 2
        yield from sorted_pairs(lo, mid)
        yield from sorted_pairs(mid + 1, hi)
        yield from merged(lo, hi, 1)


def pruned_network(n, kept):
    needed, steps = set(range(kept)), []
    for a, b in reversed(list(sorted_pairs(0, n - 1))):
        low, high = a in needed, b in needed
        if low or high:
            steps.append((a, b, low, high))
            needed |= {a, b}
    return steps[::-1]


ORDER = sorted(range(WORKERS), key=lambda w: (w // SIDE, min(w % SIDE, SIDE - w % SIDE)))
DEAL = ORDER[::-1]
NETWORK = pruned_network(DATES, KEPT)


def place():
    return lax.axis_index("date_0"), lax.axis_index("date_1"), lax.axis_index("pix")


def signal(sem, z, y, p):
    pl.semaphore_signal(sem, inc=1, device_id=(z, y, p), device_id_type=MESH)


def remote(src, dst, send, recv, z, y, p):
    return pltpu.make_async_remote_copy(
        src_ref=src, dst_ref=dst, send_sem=send, recv_sem=recv,
        device_id=(z, y, p), device_id_type=MESH,
    )


def coded(v):
    top = jnp.max(jnp.abs(v), axis=0, keepdims=True)
    e = jnp.clip(jnp.ceil(jnp.log2(jnp.maximum(top, 1e-38))), -126.0, 126.0)
    q = jnp.clip(jnp.round(v * jnp.exp2(-e) * 32767.0), -32767.0, 32767.0)
    return q.astype(jnp.int32).astype(jnp.int16), e


def lanes(i, n=LANES):
    return pl.ds(pl.multiple_of(i * n, n), n)


def kernel(
    days_ref, reflect_ref, cloud_ref, got_median, got_slope,
    day_in, xin, cin, send, part, mrow, recv, mrecv, tops,
    load_sem, own_sem, part_send, part_recv, data_send, data_recv,
    mean_send, mean_recv, relay_send, relay_recv, out_send, out_recv,
):
    z, y, p = place()
    me = z * SIDE + y
    early = z < HALF
    block = lax.rem(me, WORKERS)
    to_half = z - block // SIDE
    loads = [
        pltpu.make_async_copy(reflect_ref, xin, load_sem.at[0]),
        pltpu.make_async_copy(cloud_ref, cin, load_sem.at[1]),
        pltpu.make_async_copy(days_ref, day_in, load_sem.at[2]),
    ]
    barrier = pltpu.get_barrier_semaphore()
    shape = (BANDS, LANES)
    row = lax.broadcasted_iota(jnp.int32, shape, 0)
    lane = lax.broadcasted_iota(jnp.int32, shape, 1)

    def sized(some, sends, receives):
        return remote(some, some, sends, receives, z, y, p)

    @jax.named_scope("greet")
    def greet():
        for c in loads:
            c.start()
        for k in range(1, PEERS):
            signal(barrier, z, y, lax.rem(p + k, PEERS))

        @pl.when(early)
        def _():
            at_y = [lax.rem(y + k, SIDE) for k in range(SIDE)]

            def one(i, c):
                at_z = lax.rem(z + 2 + i, SIDE)
                for k in range(SIDE):

                    @pl.when((i != SIDE - 2) | (k != 0))
                    def _():
                        signal(barrier, at_z, at_y[k], p)

                return c

            lax.fori_loop(0, SIDE, one, 0)

    @jax.named_scope("load_wait")
    def load_wait():
        for c in loads:
            c.wait()

    @jax.named_scope("mark")
    def mark():
        def one(c, total):
            at = lanes(c)
            x = xin[:, at].astype(jnp.float32)
            clear = jnp.broadcast_to(cin[pl.ds(c, 1), :], shape) > 0
            send[:, at] = jnp.where(clear, x, sentinel).astype(jnp.bfloat16)
            return total + jnp.where(clear, x, 0.0)

        total = lax.fori_loop(0, CHUNKS, one, jnp.zeros(shape, jnp.float32), unroll=8)
        total = jnp.broadcast_to(jnp.sum(total, axis=1, keepdims=True), shape)
        clears = jnp.sum(cin[...].astype(jnp.float32), axis=0, keepdims=True)
        part[p, 0:1] = jnp.sum(jnp.where(row == lane, total, 0.0), axis=0, keepdims=True)
        part[p, 1:2] = jnp.broadcast_to(jnp.sum(clears, axis=1, keepdims=True), (1, LANES))

    @jax.named_scope("meet")
    def meet():
        @pl.when(early)
        def _():
            pl.semaphore_wait(barrier, PEERS - 1 + WORKERS - 1)

        @pl.when(jnp.logical_not(early))
        def _():
            pl.semaphore_wait(barrier, PEERS - 1 + WORKERS)

    def share(w):
        return send.at[:, lanes(w, WIDTH)]

    own = pltpu.make_async_copy(share(block), recv.at[me], own_sem)

    def to_workers(src, dst, sends, receives):
        for w in DEAL:

            @pl.when(me != w)
            def _():
                remote(src(w), dst.at[me], sends, receives, w // SIDE, w % SIDE, p).start()

    @jax.named_scope("deal")
    def deal():
        for k in range(1, PEERS):
            remote(part.at[p], part.at[p], part_send, part_recv, z, y, lax.rem(p + k, PEERS)).start()
        to_workers(share, recv, data_send, data_recv)

        @pl.when(early)
        def _():
            own.start()

    @jax.named_scope("pix_wait")
    def pix_wait():
        sized(part.at[pl.ds(0, PEERS - 1)], part_send, part_recv).wait_recv()

    @jax.named_scope("tell")
    def tell():
        sums = part[0]
        for k in range(1, PEERS):
            sums = sums + part[k]
        years = day_in[0, 0].astype(jnp.float32) * per_year
        at = lax.broadcasted_iota(jnp.int32, (1, LANES), 1)
        mrow[...] = jnp.where(at < BANDS, sums[0:1] / jnp.maximum(sums[1:2], 1.0), years)
        to_workers(lambda w: mrow, mrecv, mean_send, mean_recv)

    @jax.named_scope("data_wait")
    def data_wait():
        mrecv[me] = mrow[...]
        own.wait()
        sized(recv.at[pl.ds(0, DATES - 1)], data_send, data_recv).wait_recv()

    @jax.named_scope("medians")
    def medians():
        def one(i, c):
            at = lanes(i)
            count = jnp.zeros(shape, jnp.float32)
            xs = []
            for d in range(DATES):
                x = recv[d, :, at].astype(jnp.float32)
                count = count + jnp.where(x < 50.0, 1.0, 0.0)
                xs.append(x)
            for a, b, low, high in NETWORK:
                u, v = xs[a], xs[b]
                if low:
                    xs[a] = jnp.minimum(u, v)
                if high:
                    xs[b] = jnp.maximum(u, v)
            lower = jnp.floor((count - 1.0) * 0.5)
            upper = jnp.floor(count * 0.5)
            at_lower, at_upper = xs[0], xs[0]
            for k in range(1, KEPT):
                at_lower = jnp.where(lower == k, xs[k], at_lower)
                at_upper = jnp.where(upper == k, xs[k], at_upper)
            q, e = coded(0.5 * (at_lower + at_upper))
            got_median[block, :, at] = q
            tops[:, at] = e
            return c

        lax.fori_loop(0, WIDTH // LANES, one, 0)

    @jax.named_scope("mean_wait")
    def mean_wait():
        sized(mrecv.at[pl.ds(0, DATES - 1)], mean_send, mean_recv).wait_recv()

    @jax.named_scope("slopes")
    def slopes():
        told = mrecv[...].reshape(DATES, LANES).T
        means = told[:BANDS]
        times = told[8 : 8 + BANDS]
        zero = jnp.zeros(shape, jnp.float32)
        columns = range(WIDTH // LANES)
        state = [(zero,) * 5 for _ in columns]
        for d in range(DATES):
            mean = jnp.broadcast_to(means[:, d : d + 1], shape)
            t = jnp.broadcast_to(times[:, d : d + 1], shape)
            for i in columns:
                s0, s1, s2, sy, sty = state[i]
                x = recv[d, :, i * LANES : (i + 1) * LANES].astype(jnp.float32)
                clear = x < 50.0
                my = jnp.where(clear, x - mean, 0.0)
                mt = jnp.where(clear, t, 0.0)
                state[i] = (s0 + jnp.where(clear, 1.0, 0.0), s1 + mt, s2 + mt * t, sy + my, sty + my * t)
        for i in columns:
            s0, s1, s2, sy, sty = state[i]
            at = slice(i * LANES, (i + 1) * LANES)
            first = s0 + 1.0
            q, e = coded((first * sty - s1 * sy) / (first * (s2 + 1.0) - s1 * s1))
            ends = jnp.concatenate([e, tops[:, at]], axis=0).astype(jnp.int32).astype(jnp.int16)
            got_slope[block, 0:BANDS, at] = q
            got_slope[block, BANDS:8, at] = ends

    def relay(got, k):
        remote(got.at[block], got.at[block], relay_send.at[k], relay_recv.at[k], z + HALF, y, p).start()

    def spread(got, k):
        for w in ORDER:

            @pl.when(block != w)
            def _():
                remote(got.at[block], got.at[block], out_send.at[k], out_recv.at[k], to_half + w // SIDE, w % SIDE, p).start()

    greet()
    load_wait()
    mark()
    meet()
    deal()
    pix_wait()
    tell()
    outs = (got_median, got_slope)

    @pl.when(early)
    def _():
        data_wait()
        medians()
        with jax.named_scope("spread0"):
            relay(outs[0], 0)
            spread(outs[0], 0)
        mean_wait()
        slopes()
        with jax.named_scope("spread1"):
            relay(outs[1], 1)
            spread(outs[1], 1)

    @pl.when(jnp.logical_not(early))
    def _():
        for k, got in enumerate(outs):
            with jax.named_scope(f"relay{k}"):
                sized(got.at[block], relay_send.at[k], relay_recv.at[k]).wait_recv()
            with jax.named_scope(f"spread{k}"):
                spread(got, k)

    for k, got in enumerate(outs):
        with jax.named_scope(f"out_wait{k}"):
            sized(got.at[pl.ds(0, WORKERS - 1)], out_send.at[k], out_recv.at[k]).wait_recv()

    with jax.named_scope("drain"):
        sized(part.at[pl.ds(0, PEERS - 1)], part_send, part_recv).wait_send()

        def sent(n):
            sized(recv.at[pl.ds(0, n)], data_send, data_recv).wait_send()
            sized(mrecv.at[pl.ds(0, n)], mean_send, mean_recv).wait_send()

        @pl.when(early)
        def _():
            sent(WORKERS - 1)
            for k, got in enumerate(outs):
                sized(got.at[block], relay_send.at[k], relay_recv.at[k]).wait_send()

        @pl.when(jnp.logical_not(early))
        def _():
            sent(WORKERS)

        for k, got in enumerate(outs):
            sized(got.at[pl.ds(0, WORKERS - 1)], out_send.at[k], out_recv.at[k]).wait_send()


def finish(got_median, got_slope, median_ref, slope_ref):
    def one(w, c):
        at = lanes(w, WIDTH)
        slope = got_slope[w].astype(jnp.int32).astype(jnp.float32)
        scale = jnp.exp2(slope[BANDS:8]) * (1.0 / 32767.0)
        median_ref[:, at] = got_median[w].astype(jnp.int32).astype(jnp.float32) * scale[1:2]
        slope_ref[:, at] = slope[:BANDS] * scale[0:1]
        return c

    lax.fori_loop(0, WORKERS, one, 0, unroll=4)


def local(reflect, cloud_free, days):
    whole = pl.BlockSpec(memory_space=pltpu.VMEM)
    far = pl.BlockSpec(memory_space=pltpu.HBM)
    out = jax.ShapeDtypeStruct((BANDS, TILE), jnp.float32)
    dma = pltpu.SemaphoreType.DMA
    got = pl.pallas_call(
        kernel,
        out_shape=(
            jax.ShapeDtypeStruct((WORKERS, BANDS, WIDTH), jnp.int16),
            jax.ShapeDtypeStruct((WORKERS, 8, WIDTH), jnp.int16),
        ),
        in_specs=[far, far, far],
        out_specs=(whole, whole),
        scratch_shapes=[
            pltpu.SMEM((1, 1), jnp.int32),
            pltpu.VMEM((BANDS, TILE), jnp.bfloat16),
            pltpu.VMEM((CHUNKS, LANES), jnp.int32),
            pltpu.VMEM((BANDS, TILE), jnp.bfloat16),
            pltpu.VMEM((PEERS, 2, LANES), jnp.float32),
            pltpu.VMEM((1, LANES), jnp.float32),
            pltpu.VMEM((DATES, BANDS, WIDTH), jnp.bfloat16),
            pltpu.VMEM((DATES, 1, LANES), jnp.float32),
            pltpu.VMEM((1, WIDTH), jnp.float32),
            dma((3,)), dma, dma, dma, dma, dma, dma, dma,
            dma((2,)), dma((2,)), dma((2,)), dma((2,)),
        ],
        compiler_params=pltpu.CompilerParams(
            collective_id=0, has_side_effects=True, vmem_limit_bytes=8 * 2**20
        ),
    )(
        days.reshape(1, 1),
        *(
            pltpu.with_memory_space_constraint(a, pltpu.HBM)
            for a in (reflect.reshape(BANDS, TILE), cloud_free.reshape(CHUNKS, LANES))
        ),
    )
    return pl.pallas_call(
        finish, out_shape=(out, out), in_specs=[whole, whole], out_specs=(whole, whole),
        compiler_params=pltpu.CompilerParams(vmem_limit_bytes=4 * 2**20),
    )(*got)


def solution(mesh):
    torus = Mesh(mesh.devices.reshape(SIDE, SIDE, mesh.shape["pix"]), ("date_0", "date_1", "pix"))
    return jax.shard_map(
        local,
        mesh=torus,
        in_specs=(P(DATE, None, "pix"), P(DATE, "pix"), P(DATE)),
        out_specs=(P(None, "pix"), P(None, "pix")),
        check_vma=False,
    )
```

time: 149 us -> 34 us (0.23)
  the two profiles are of different devices: /device:TPU:8 before, /device:TPU:1 now
where the time goes in v1:
time: 34 us; the launch traced here: 33.9 us
  Pallas kernels  32.6 us (96%)
  between operations  1.28 us (4%)
    pallas_call x1, Pallas kernels, local(): pl.pallas_call(kernel, out_shape=(jax.ShapeDtypeStruct((WORKERS, BANDS, W...  31.7 us
    pallas_call x1, Pallas kernels, local(): pl.pallas_call(finish, out_shape=(out, out), in_specs=[whole, whole], out...  0.95 us

profile of v1, /device:TPU:1, one launch (start us, length us, event | category | flops | bytes accessed | tf_op | source)
XLA Modules:
  0.0 33.9 jit_solution(14866424061573802825)
XLA Ops:
  1.3 31.7 %shard_map.50 = (s16[32,6,256]{2,1,0:T(8,128)(2,1)S(1)}, s16[32,8,256]{2,1,0:T(8,128)(2,1)S(1)}) custom-call(s32[1,1]{1,0:T(1,128)} %bitcast.3.days_ref, bf16[6,8192]{1,0:T(8,128)(2,1)} %bitcast.4, s32[64,128]{1,0:T(8,128)} %bitcast.5), custom_call_target="tpu_custom_call" | custom-call | tf_op jit(solution)/shard_map/pallas_call | solution.py:348
  32.9 1.0 %shard_map.51 = (f32[6,8192]{1,0:T(8,128)}, f32[6,8192]{1,0:T(8,128)}) custom-call(s16[32,6,256]{2,1,0:T(8,128)(2,1)S(1)} %get-tuple-element.4.got_median, s16[32,8,256]{2,1,0:T(8,128)(2,1)S(1)} %get-tuple-element.5.got_slope), custom_call_target="tpu_custom_call" | custom-call | tf_op jit(solution)/shard_map/pallas_call | solution.py:379

commit v2 on v1

--- a/solution.py
+++ b/solution.py
@@ -15,8 +15,9 @@
 PEERS = 8
 LANES = 128
 TILE = 8192
-HALF = SIDE // 2
-WORKERS = HALF * SIDE
+WORKERS = 32
+PLACE = [0, 1, 2, 3, 8, 9, 6, 7, 5, 10, 16, 4, 17, 11, 14, 15, 18, 24, 13, 12, 19, 23, 25, 22, 26, 21, 20, 31, 32, 30, 40, 48]
+PARTNER = [50, 49, 58, 51, 56, 57, 54, 55, 61, 27, 45, 52, 44, 59, 62, 63, 35, 33, 53, 60, 43, 29, 41, 38, 34, 37, 36, 46, 39, 28, 42, 47]
 WIDTH = TILE // WORKERS
 CHUNKS = TILE // LANES
 BANDS = 6
@@ -53,8 +54,8 @@
     return steps[::-1]
 
 
-ORDER = sorted(range(WORKERS), key=lambda w: (w // SIDE, min(w % SIDE, SIDE - w % SIDE)))
-DEAL = ORDER[::-1]
+LATE = [27, 29, 33, 41, 34, 28, 56, 50, 49, 35, 42, 39, 57, 38, 58, 43, 47, 51, 37, 46, 55, 36, 54, 45, 59, 63, 44, 53, 62, 52, 61, 60]
+FIRST = 24
 NETWORK = pruned_network(DATES, KEPT)
 
 
@@ -77,7 +78,15 @@
     top = jnp.max(jnp.abs(v), axis=0, keepdims=True)
     e = jnp.clip(jnp.ceil(jnp.log2(jnp.maximum(top, 1e-38))), -126.0, 126.0)
     q = jnp.clip(jnp.round(v * jnp.exp2(-e) * 32767.0), -32767.0, 32767.0)
-    return q.astype(jnp.int32).astype(jnp.int16), e
+    return q, e
+
+
+def narrow(q):
+    return q.astype(jnp.int32).astype(jnp.int16)
+
+
+def split(ab, c):
+    return [jnp.concatenate([ab[4 * i : 4 * i + 4], c[2 * i : 2 * i + 2]], axis=0) for i in range(2)]
 
 
 def lanes(i, n=LANES):
@@ -92,9 +101,12 @@
 ):
     z, y, p = place()
     me = z * SIDE + y
-    early = z < HALF
-    block = lax.rem(me, WORKERS)
-    to_half = z - block // SIDE
+    early = (z < 3) | ((z == 3) & ((y < 3) | (y > 5))) | ((y == 0) & (z < 7))
+    block, pair = jnp.int32(0), jnp.int32(0)
+    for w in range(1, WORKERS):
+        block = jnp.where((me == PLACE[w]) | (me == PARTNER[w]), w, block)
+    for w in range(WORKERS):
+        pair = jnp.where(me == PLACE[w], PARTNER[w], pair)
     loads = [
         pltpu.make_async_copy(reflect_ref, xin, load_sem.at[0]),
         pltpu.make_async_copy(cloud_ref, cin, load_sem.at[1]),
@@ -104,6 +116,7 @@
     shape = (BANDS, LANES)
     row = lax.broadcasted_iota(jnp.int32, shape, 0)
     lane = lax.broadcasted_iota(jnp.int32, shape, 1)
+    band = jnp.where(lane < 4, lane, jnp.where(lane < 10, lane - 4, lane - 6))
 
     def sized(some, sends, receives):
         return remote(some, some, sends, receives, z, y, p)
@@ -138,17 +151,21 @@
 
     @jax.named_scope("mark")
     def mark():
-        def one(c, total):
-            at = lanes(c)
-            x = xin[:, at].astype(jnp.float32)
-            clear = jnp.broadcast_to(cin[pl.ds(c, 1), :], shape) > 0
-            send[:, at] = jnp.where(clear, x, sentinel).astype(jnp.bfloat16)
-            return total + jnp.where(clear, x, 0.0)
-
-        total = lax.fori_loop(0, CHUNKS, one, jnp.zeros(shape, jnp.float32), unroll=8)
+        def one(w, total):
+            for i in range(2):
+                c = 2 * w + i
+                x = xin[:, lanes(c)].astype(jnp.float32)
+                clear = jnp.broadcast_to(cin[pl.ds(c, 1), :], shape) > 0
+                marked = jnp.where(clear, x, sentinel).astype(jnp.bfloat16)
+                send[w, i] = marked[:4]
+                send[w, 2, 2 * i : 2 * i + 2] = marked[4:]
+                total = total + jnp.where(clear, x, 0.0)
+            return total
+
+        total = lax.fori_loop(0, WORKERS, one, jnp.zeros(shape, jnp.float32), unroll=4)
         total = jnp.broadcast_to(jnp.sum(total, axis=1, keepdims=True), shape)
         clears = jnp.sum(cin[...].astype(jnp.float32), axis=0, keepdims=True)
-        part[p, 0:1] = jnp.sum(jnp.where(row == lane, total, 0.0), axis=0, keepdims=True)
+        part[p, 0:1] = jnp.sum(jnp.where(row == band, total, 0.0), axis=0, keepdims=True)
         part[p, 1:2] = jnp.broadcast_to(jnp.sum(clears, axis=1, keepdims=True), (1, LANES))
 
     @jax.named_scope("meet")
@@ -162,16 +179,16 @@
             pl.semaphore_wait(barrier, PEERS - 1 + WORKERS)
 
     def share(w):
-        return send.at[:, lanes(w, WIDTH)]
+        return send.at[w]
 
     own = pltpu.make_async_copy(share(block), recv.at[me], own_sem)
 
     def to_workers(src, dst, sends, receives):
-        for w in DEAL:
-
-            @pl.when(me != w)
+        for w in reversed(range(WORKERS)):
+
+            @pl.when(me != PLACE[w])
             def _():
-                remote(src(w), dst.at[me], sends, receives, w // SIDE, w % SIDE, p).start()
+                remote(src(w), dst.at[me], sends, receives, PLACE[w] // SIDE, PLACE[w] % SIDE, p).start()
 
     @jax.named_scope("deal")
     def deal():
@@ -194,7 +211,7 @@
             sums = sums + part[k]
         years = day_in[0, 0].astype(jnp.float32) * per_year
         at = lax.broadcasted_iota(jnp.int32, (1, LANES), 1)
-        mrow[...] = jnp.where(at < BANDS, sums[0:1] / jnp.maximum(sums[1:2], 1.0), years)
+        mrow[...] = jnp.where(at < 12, sums[0:1] / jnp.maximum(sums[1:2], 1.0), years)
         to_workers(lambda w: mrow, mrecv, mean_send, mean_recv)
 
     @jax.named_scope("data_wait")
@@ -203,14 +220,19 @@
         own.wait()
         sized(recv.at[pl.ds(0, DATES - 1)], data_send, data_recv).wait_recv()
 
+    def first_bands(d):
+        return jnp.concatenate([recv[d, i].astype(jnp.float32) for i in range(2)], axis=0)
+
+    def last_bands(d):
+        return recv[d, 2].astype(jnp.float32)
+
     @jax.named_scope("medians")
     def medians():
-        def one(i, c):
-            at = lanes(i)
-            count = jnp.zeros(shape, jnp.float32)
-            xs = []
+        picked = []
+        for piece in (first_bands, last_bands):
+            count, xs = 0.0, []
             for d in range(DATES):
-                x = recv[d, :, at].astype(jnp.float32)
+                x = piece(d)
                 count = count + jnp.where(x < 50.0, 1.0, 0.0)
                 xs.append(x)
             for a, b, low, high in NETWORK:
@@ -225,12 +247,12 @@
             for k in range(1, KEPT):
                 at_lower = jnp.where(lower == k, xs[k], at_lower)
                 at_upper = jnp.where(upper == k, xs[k], at_upper)
-            q, e = coded(0.5 * (at_lower + at_upper))
-            got_median[block, :, at] = q
-            tops[:, at] = e
-            return c
-
-        lax.fori_loop(0, WIDTH // LANES, one, 0)
+            picked.append(0.5 * (at_lower + at_upper))
+        for i, v in enumerate(split(*picked)):
+            q, e = coded(v)
+            got_median[block, i] = narrow(q[:4])
+            got_median[block, 2, 2 * i : 2 * i + 2] = narrow(q[4:])
+            tops[:, i * LANES : (i + 1) * LANES] = e
 
     @jax.named_scope("mean_wait")
     def mean_wait():
@@ -239,39 +261,39 @@
     @jax.named_scope("slopes")
     def slopes():
         told = mrecv[...].reshape(DATES, LANES).T
-        means = told[:BANDS]
-        times = told[8 : 8 + BANDS]
-        zero = jnp.zeros(shape, jnp.float32)
-        columns = range(WIDTH // LANES)
-        state = [(zero,) * 5 for _ in columns]
-        for d in range(DATES):
-            mean = jnp.broadcast_to(means[:, d : d + 1], shape)
-            t = jnp.broadcast_to(times[:, d : d + 1], shape)
-            for i in columns:
-                s0, s1, s2, sy, sty = state[i]
-                x = recv[d, :, i * LANES : (i + 1) * LANES].astype(jnp.float32)
+        made = []
+        for piece, at, rows in ((first_bands, 0, 8), (last_bands, 8, 4)):
+            s0 = s1 = s2 = sy = sty = jnp.zeros((rows, LANES), jnp.float32)
+            for d in range(DATES):
+                x = piece(d)
+                mean = jnp.broadcast_to(told[at : at + rows, d : d + 1], x.shape)
+                t = jnp.broadcast_to(told[16 : 16 + rows, d : d + 1], x.shape)
                 clear = x < 50.0
                 my = jnp.where(clear, x - mean, 0.0)
                 mt = jnp.where(clear, t, 0.0)
-                state[i] = (s0 + jnp.where(clear, 1.0, 0.0), s1 + mt, s2 + mt * t, sy + my, sty + my * t)
-        for i in columns:
-            s0, s1, s2, sy, sty = state[i]
-            at = slice(i * LANES, (i + 1) * LANES)
+                s0 = s0 + jnp.where(clear, 1.0, 0.0)
+                s1 = s1 + mt
+                s2 = s2 + mt * t
+                sy = sy + my
+                sty = sty + my * t
             first = s0 + 1.0
-            q, e = coded((first * sty - s1 * sy) / (first * (s2 + 1.0) - s1 * s1))
-            ends = jnp.concatenate([e, tops[:, at]], axis=0).astype(jnp.int32).astype(jnp.int16)
-            got_slope[block, 0:BANDS, at] = q
-            got_slope[block, BANDS:8, at] = ends
+            made.append((first * sty - s1 * sy) / (first * (s2 + 1.0) - s1 * s1))
+        for i, v in enumerate(split(*made)):
+            q, e = coded(v)
+            got_slope[block, i] = narrow(q[:4])
+            got_slope[block, 2, 2 * i : 2 * i + 2] = narrow(q[4:])
+            ends = jnp.concatenate([e, tops[:, i * LANES : (i + 1) * LANES]], axis=0)
+            got_slope[block, 3, 2 * i : 2 * i + 2] = narrow(ends)
 
     def relay(got, k):
-        remote(got.at[block], got.at[block], relay_send.at[k], relay_recv.at[k], z + HALF, y, p).start()
-
-    def spread(got, k):
-        for w in ORDER:
-
-            @pl.when(block != w)
+        remote(got.at[block], got.at[block], relay_send.at[k], relay_recv.at[k], pair // SIDE, lax.rem(pair, SIDE), p).start()
+
+    def spread(got, k, group):
+        for to in group:
+
+            @pl.when(me != to)
             def _():
-                remote(got.at[block], got.at[block], out_send.at[k], out_recv.at[k], to_half + w // SIDE, w % SIDE, p).start()
+                remote(got.at[block], got.at[block], out_send.at[k], out_recv.at[k], to // SIDE, to % SIDE, p).start()
 
     greet()
     load_wait()
@@ -288,12 +310,14 @@
         medians()
         with jax.named_scope("spread0"):
             relay(outs[0], 0)
-            spread(outs[0], 0)
+            spread(outs[0], 0, PLACE[:FIRST])
         mean_wait()
         slopes()
         with jax.named_scope("spread1"):
             relay(outs[1], 1)
-            spread(outs[1], 1)
+            spread(outs[1], 1, PLACE[:FIRST])
+            spread(outs[0], 0, PLACE[FIRST:])
+            spread(outs[1], 1, PLACE[FIRST:])
 
     @pl.when(jnp.logical_not(early))
     def _():
@@ -301,7 +325,7 @@
             with jax.named_scope(f"relay{k}"):
                 sized(got.at[block], relay_send.at[k], relay_recv.at[k]).wait_recv()
             with jax.named_scope(f"spread{k}"):
-                spread(got, k)
+                spread(got, k, LATE)
 
     for k, got in enumerate(outs):
         with jax.named_scope(f"out_wait{k}"):
@@ -330,11 +354,13 @@
 
 def finish(got_median, got_slope, median_ref, slope_ref):
     def one(w, c):
-        at = lanes(w, WIDTH)
-        slope = got_slope[w].astype(jnp.int32).astype(jnp.float32)
-        scale = jnp.exp2(slope[BANDS:8]) * (1.0 / 32767.0)
-        median_ref[:, at] = got_median[w].astype(jnp.int32).astype(jnp.float32) * scale[1:2]
-        slope_ref[:, at] = slope[:BANDS] * scale[0:1]
+        scale = jnp.exp2(got_slope[w, 3].astype(jnp.int32).astype(jnp.float32)) * (1.0 / 32767.0)
+        for k, (got, ref) in enumerate(((got_slope, slope_ref), (got_median, median_ref))):
+            for i in range(2):
+                at, by = lanes(2 * w + i), scale[2 * i + k : 2 * i + k + 1]
+                some = slice(2 * i, 2 * i + 2)
+                ref[:4, at] = got[w, i].astype(jnp.int32).astype(jnp.float32) * by
+                ref[4:, at] = got[w, 2, some].astype(jnp.int32).astype(jnp.float32) * by
         return c
 
     lax.fori_loop(0, WORKERS, one, 0, unroll=4)
@@ -348,8 +374,8 @@
     got = pl.pallas_call(
         kernel,
         out_shape=(
-            jax.ShapeDtypeStruct((WORKERS, BANDS, WIDTH), jnp.int16),
-            jax.ShapeDtypeStruct((WORKERS, 8, WIDTH), jnp.int16),
+            jax.ShapeDtypeStruct((WORKERS, 3, 4, LANES), jnp.int16),
+            jax.ShapeDtypeStruct((WORKERS, 4, 4, LANES), jnp.int16),
         ),
         in_specs=[far, far, far],
         out_specs=(whole, whole),
@@ -357,10 +383,10 @@
             pltpu.SMEM((1, 1), jnp.int32),
             pltpu.VMEM((BANDS, TILE), jnp.bfloat16),
             pltpu.VMEM((CHUNKS, LANES), jnp.int32),
-            pltpu.VMEM((BANDS, TILE), jnp.bfloat16),
+            pltpu.VMEM((WORKERS, 3, 4, LANES), jnp.bfloat16),
             pltpu.VMEM((PEERS, 2, LANES), jnp.float32),
             pltpu.VMEM((1, LANES), jnp.float32),
-            pltpu.VMEM((DATES, BANDS, WIDTH), jnp.bfloat16),
+            pltpu.VMEM((DATES, 3, 4, LANES), jnp.bfloat16),
             pltpu.VMEM((DATES, 1, LANES), jnp.float32),
             pltpu.VMEM((1, WIDTH), jnp.float32),
             dma((3,)), dma, dma, dma, dma, dma, dma, dma,

time: 34 us -> 32.7 us (0.962)
  the two profiles are of different devices: /device:TPU:1 before, /device:TPU:128 now
where the time goes in v2:
time: 32.7 us; the launch traced here: 32.6 us
  Pallas kernels  31.3 us (96%)
  between operations  1.28 us (4%)
    pallas_call x1, Pallas kernels, local(): pl.pallas_call(kernel, out_shape=(jax.ShapeDtypeStruct((WORKERS, 3, 4, LA...  30.3 us
    pallas_call x1, Pallas kernels, local(): pl.pallas_call(finish, out_shape=(out, out), in_specs=[whole, whole], out...  1 us

profile of v2, /device:TPU:128, one launch (start us, length us, event | category | flops | bytes accessed | tf_op | source)
XLA Modules:
  0.0 32.6 jit_solution(6413320711931093362)
XLA Ops:
  1.3 30.3 %shard_map.50 = (s16[32,3,4,128]{3,2,1,0:T(4,128)(2,1)S(1)}, s16[32,4,4,128]{3,2,1,0:T(4,128)(2,1)S(1)}) custom-call(s32[1,1]{1,0:T(1,128)} %bitcast.3.days_ref, bf16[6,8192]{1,0:T(8,128)(2,1)} %bitcast.4, s32[64,128]{1,0:T(8,128)} %bitcast.5), custom_call_target="tpu_custom_call" | custom-call | tf_op jit(solution)/shard_map/pallas_call | solution.py:374
  31.6 1.0 %shard_map.51 = (f32[6,8192]{1,0:T(8,128)}, f32[6,8192]{1,0:T(8,128)}) custom-call(s16[32,3,4,128]{3,2,1,0:T(4,128)(2,1)S(1)} %get-tuple-element.4.got_median, s16[32,4,4,128]{3,2,1,0:T(4,128)(2,1)S(1)} %get-tuple-element.5.got_slope), custom_call_target="tpu_custom_call" | custom-call | tf_op jit(solution)/shard_map/pallas_call | solution.py:405

commit v3 on v2

--- a/solution.py
+++ b/solution.py
@@ -16,8 +16,8 @@
 LANES = 128
 TILE = 8192
 WORKERS = 32
-PLACE = [0, 1, 2, 3, 8, 9, 6, 7, 5, 10, 16, 4, 17, 11, 14, 15, 18, 24, 13, 12, 19, 23, 25, 22, 26, 21, 20, 31, 32, 30, 40, 48]
-PARTNER = [50, 49, 58, 51, 56, 57, 54, 55, 61, 27, 45, 52, 44, 59, 62, 63, 35, 33, 53, 60, 43, 29, 41, 38, 34, 37, 36, 46, 39, 28, 42, 47]
+PLACE = [0, 1, 2, 3, 8, 9, 6, 7, 5, 10, 16, 4, 17, 11, 14, 15, 18, 24, 13, 12, 19, 23, 25, 22, 26, 21, 20, 27, 31, 32, 30, 40]
+PARTNER = [48, 49, 50, 51, 56, 57, 54, 55, 61, 58, 45, 52, 43, 59, 62, 63, 34, 41, 53, 60, 36, 39, 33, 38, 35, 37, 28, 44, 29, 47, 46, 42]
 WIDTH = TILE // WORKERS
 CHUNKS = TILE // LANES
 BANDS = 6
@@ -54,7 +54,7 @@
     return steps[::-1]
 
 
-LATE = [27, 29, 33, 41, 34, 28, 56, 50, 49, 35, 42, 39, 57, 38, 58, 43, 47, 51, 37, 46, 55, 36, 54, 45, 59, 63, 44, 53, 62, 52, 61, 60]
+LATE = [48, 29, 33, 34, 41, 28, 56, 50, 49, 35, 42, 39, 57, 38, 58, 43, 47, 51, 37, 46, 55, 36, 54, 45, 59, 63, 44, 53, 62, 52, 61, 60]
 FIRST = 24
 NETWORK = pruned_network(DATES, KEPT)
 
@@ -101,7 +101,7 @@
 ):
     z, y, p = place()
     me = z * SIDE + y
-    early = (z < 3) | ((z == 3) & ((y < 3) | (y > 5))) | ((y == 0) & (z < 7))
+    early = (z < 3) | ((z == 3) & ((y < 4) | (y > 5))) | ((y == 0) & (z < 6))
     block, pair = jnp.int32(0), jnp.int32(0)
     for w in range(1, WORKERS):
         block = jnp.where((me == PLACE[w]) | (me == PARTNER[w]), w, block)

time: 32.7 us -> 32.2 us (0.985)
  the two profiles are of different devices: /device:TPU:128 before, /device:TPU:8 now
where the time goes in v3:
time: 32.2 us; the launch traced here: 32.1 us
  Pallas kernels  30.8 us (96%)
  between operations  1.28 us (4%)
    pallas_call x1, Pallas kernels, local(): pl.pallas_call(kernel, out_shape=(jax.ShapeDtypeStruct((WORKERS, 3, 4, LA...  29.8 us
    pallas_call x1, Pallas kernels, local(): pl.pallas_call(finish, out_shape=(out, out), in_specs=[whole, whole], out...  1 us

profile of v3, /device:TPU:8, one launch (start us, length us, event | category | flops | bytes accessed | tf_op | source)
XLA Modules:
  0.0 32.1 jit_solution(3782607755697965413)
XLA Ops:
  1.3 29.8 %shard_map.50 = (s16[32,3,4,128]{3,2,1,0:T(4,128)(2,1)S(1)}, s16[32,4,4,128]{3,2,1,0:T(4,128)(2,1)S(1)}) custom-call(s32[1,1]{1,0:T(1,128)} %bitcast.3.days_ref, bf16[6,8192]{1,0:T(8,128)(2,1)} %bitcast.4, s32[64,128]{1,0:T(8,128)} %bitcast.5), custom_call_target="tpu_custom_call" | custom-call | tf_op jit(solution)/shard_map/pallas_call | solution.py:374
  31.1 1.0 %shard_map.51 = (f32[6,8192]{1,0:T(8,128)}, f32[6,8192]{1,0:T(8,128)}) custom-call(s16[32,3,4,128]{3,2,1,0:T(4,128)(2,1)S(1)} %get-tuple-element.4.got_median, s16[32,4,4,128]{3,2,1,0:T(4,128)(2,1)S(1)} %get-tuple-element.5.got_slope), custom_call_target="tpu_custom_call" | custom-call | tf_op jit(solution)/shard_map/pallas_call | solution.py:405

commit v4 on v3

--- a/solution.py
+++ b/solution.py
@@ -133,10 +133,10 @@
             at_y = [lax.rem(y + k, SIDE) for k in range(SIDE)]
 
             def one(i, c):
-                at_z = lax.rem(z + 2 + i, SIDE)
+                at_z = lax.rem(z + 3 + i, SIDE)
                 for k in range(SIDE):
 
-                    @pl.when((i != SIDE - 2) | (k != 0))
+                    @pl.when((i != SIDE - 3) | (k != 0))
                     def _():
                         signal(barrier, at_z, at_y[k], p)
 
@@ -261,21 +261,20 @@
     @jax.named_scope("slopes")
     def slopes():
         told = mrecv[...].reshape(DATES, LANES).T
-        made = []
-        for piece, at, rows in ((first_bands, 0, 8), (last_bands, 8, 4)):
-            s0 = s1 = s2 = sy = sty = jnp.zeros((rows, LANES), jnp.float32)
-            for d in range(DATES):
-                x = piece(d)
+        pieces = ((first_bands, 0, 8), (last_bands, 8, 4))
+        state = [(jnp.zeros((rows, LANES), jnp.float32),) * 5 for _, _, rows in pieces]
+        for d in range(DATES):
+            times = jnp.broadcast_to(told[16:24, d : d + 1], (8, LANES))
+            for k, (piece, at, rows) in enumerate(pieces):
+                s0, s1, s2, sy, sty = state[k]
+                x, t = piece(d), times[:rows]
                 mean = jnp.broadcast_to(told[at : at + rows, d : d + 1], x.shape)
-                t = jnp.broadcast_to(told[16 : 16 + rows, d : d + 1], x.shape)
                 clear = x < 50.0
                 my = jnp.where(clear, x - mean, 0.0)
                 mt = jnp.where(clear, t, 0.0)
-                s0 = s0 + jnp.where(clear, 1.0, 0.0)
-                s1 = s1 + mt
-                s2 = s2 + mt * t
-                sy = sy + my
-                sty = sty + my * t
+                state[k] = (s0 + jnp.where(clear, 1.0, 0.0), s1 + mt, s2 + mt * t, sy + my, sty + my * t)
+        made = []
+        for s0, s1, s2, sy, sty in state:
             first = s0 + 1.0
             made.append((first * sty - s1 * sy) / (first * (s2 + 1.0) - s1 * s1))
         for i, v in enumerate(split(*made)):

time: 32.2 us -> 32.1 us (level)
  no operation moved by 1% of the time
where the time goes in v4:
time: 32.1 us; the launch traced here: 32 us
  Pallas kernels  30.7 us (96%)
  between operations  1.28 us (4%)
    pallas_call x1, Pallas kernels, local(): pl.pallas_call(kernel, out_shape=(jax.ShapeDtypeStruct((WORKERS, 3, 4, LA...  29.7 us
    pallas_call x1, Pallas kernels, local(): pl.pallas_call(finish, out_shape=(out, out), in_specs=[whole, whole], out...  1 us

profile of v4, /device:TPU:8, one launch (start us, length us, event | category | flops | bytes accessed | tf_op | source)
XLA Modules:
  0.0 32.0 jit_solution(8750495341698012248)
XLA Ops:
  1.3 29.7 %shard_map.50 = (s16[32,3,4,128]{3,2,1,0:T(4,128)(2,1)S(1)}, s16[32,4,4,128]{3,2,1,0:T(4,128)(2,1)S(1)}) custom-call(s32[1,1]{1,0:T(1,128)} %bitcast.3.days_ref, bf16[6,8192]{1,0:T(8,128)(2,1)} %bitcast.4, s32[64,128]{1,0:T(8,128)} %bitcast.5), custom_call_target="tpu_custom_call" | custom-call | tf_op jit(solution)/shard_map/pallas_call | solution.py:373
  31.0 1.0 %shard_map.51 = (f32[6,8192]{1,0:T(8,128)}, f32[6,8192]{1,0:T(8,128)}) custom-call(s16[32,3,4,128]{3,2,1,0:T(4,128)(2,1)S(1)} %get-tuple-element.4.got_median, s16[32,4,4,128]{3,2,1,0:T(4,128)(2,1)S(1)} %get-tuple-element.5.got_slope), custom_call_target="tpu_custom_call" | custom-call | tf_op jit(solution)/shard_map/pallas_call | solution.py:404
